TPU v7x, 32 devices: a whole 2x2x4 slice. The times are simulated.
32 devices in a mesh: pipe: 4 (over y, x), dp: 8 (over z, core).
Axes of the slice: x: 2, y: 2, z: 4, core: 2. Of those that a mesh axis runs over, the one named last changes fastest.
Arguments:
- acts: bfloat16 [4, 2048, 3072], P('pipe', 'dp'), may hold values from -24 to 24, as said below
- grad: float32 [12288, 4096], P('pipe', 'dp'), may hold values from -6 to 6
- owner_of: int32 [4, 12], replicated, may hold values from 0 to 3, as said below
Outputs:
- precond: float32 [12288, 4096], P('pipe', 'dp')
- held_inverse: float32 [4, 24, 256, 256], P('pipe', None, 'dp')
Inputs may be any that keep to these rules, and one draw needn't show every extreme that they name: `acts`: column and token scales of the activations vary; entries lie within the range. `owner_of`: no section index owns more than 24 blocks in all, and some section index owns exactly 24.
All inputs are finite; a program needn't handle non-finite values.
Results may differ from a plain program's by a relative error of at most 0.0003.
Values sent between devices are 32-bit elements; how exact they have to be, the bound alone decides.
A program may use at most 128 MiB of HBM per device.

v0:
```python
import jax
import jax.numpy as jnp
from jax import lax
from jax.sharding import PartitionSpec as P

BLK = 256
HOST = 24
damping_ratio = 0.1


def invert_blocks(factor, vacant):
    order_size = factor.shape[-1]
    diagonal_sum = jnp.sum(jnp.diagonal(factor, axis1=1, axis2=2), axis=1)
    damping = damping_ratio * diagonal_sum / order_size
    identity = jnp.eye(order_size, dtype=factor.dtype)
    shifted = factor + (damping + vacant)[:, None, None] * identity
    cholesky_lower = jnp.linalg.cholesky(shifted)
    identity_stack = jnp.broadcast_to(identity, factor.shape)
    inv_lower = lax.linalg.triangular_solve(
        cholesky_lower, identity_stack, left_side=True, lower=True
    )
    return jnp.einsum("mkr,mkc->mrc", inv_lower, inv_lower, precision=lax.Precision.HIGHEST)


def slot_tables(owner_of):
    owners_flat = owner_of.reshape(-1)
    positions = jnp.arange(owners_flat.shape[0], dtype=jnp.int32)
    matches = owners_flat[:, None] == owners_flat[None, :]
    before = positions[None, :] < positions[:, None]
    slot_rank = jnp.sum((matches & before).astype(jnp.int32), axis=1)
    return (owners_flat, slot_rank)


def shards(acts, grad, owner_of):
    tokens = acts.shape[1]
    feature_count = acts.shape[2]
    nblocks = feature_count // BLK
    data_count = lax.axis_size("dp")
    section_count = lax.axis_size("pipe")
    row_share = BLK // data_count
    all_tokens = tokens * data_count
    section_index = lax.axis_index("pipe")
    member = lax.axis_index("dp")
    features = acts[0].reshape(tokens, nblocks, BLK)
    owners_flat, slot_rank = slot_tables(owner_of)
    slot_ids = jnp.arange(HOST, dtype=jnp.int32)
    pick_mine = (
        (owners_flat[None, :] == section_index) & (slot_rank[None, :] == slot_ids[:, None])
    ).astype(jnp.float32)
    own_owners = lax.dynamic_index_in_dim(owner_of, section_index, 0, keepdims=False)
    own_ranks = lax.dynamic_index_in_dim(
        slot_rank.reshape(section_count, nblocks), section_index, 0, keepdims=False
    )
    target = own_owners * HOST + own_ranks
    pick_back = (
        jnp.arange(section_count * HOST, dtype=jnp.int32)[None, :] == target[:, None]
    ).astype(jnp.float32)
    block_terms = jnp.einsum("tbr,tbc->rbc", features, features, preferred_element_type=jnp.float32)
    my_rows = lax.psum_scatter(
        block_terms.reshape(row_share * lax.axis_size("dp"), nblocks * BLK),
        "dp",
        scatter_dimension=0,
        tiled=True,
    )
    pieces = lax.all_gather(my_rows, "pipe", axis=0, tiled=True).reshape(
        section_count, row_share, nblocks, BLK
    )
    hosted = jnp.einsum(
        "jsb,srbc->jrc",
        pick_mine.reshape(HOST, section_count, nblocks),
        pieces,
        precision=lax.Precision.HIGHEST,
    )
    occupied = jnp.sum(pick_mine, axis=1)
    per_member = (HOST + data_count - 1) // data_count
    padded_count = per_member * data_count
    padded = jnp.pad(hosted, ((0, padded_count - HOST), (0, 0), (0, 0)))
    mine_blocks = lax.all_to_all(padded, "dp", split_axis=0, concat_axis=1, tiled=True) / all_tokens
    padded_flags = jnp.pad(occupied, (0, padded_count - HOST))
    held_flags = lax.dynamic_slice_in_dim(padded_flags, member * per_member, per_member, 0)
    inverted = invert_blocks(mine_blocks, 1.0 - held_flags) * held_flags[:, None, None]
    spread_rows = lax.all_to_all(inverted, "dp", split_axis=1, concat_axis=0, tiled=True)
    held_rows = spread_rows[:HOST]
    returned = lax.all_gather(held_rows, "pipe", axis=0, tiled=True)
    own_rows = jnp.einsum("bm,mrc->brc", pick_back, returned, precision=lax.Precision.HIGHEST)
    inverse = lax.all_gather(own_rows, "dp", axis=1, tiled=True)
    grad_blocks = grad.reshape(nblocks, BLK, grad.shape[1])
    precond = jnp.einsum("brk,bkc->brc", inverse, grad_blocks, precision=lax.Precision.HIGHEST)
    return (precond.reshape(feature_count, grad.shape[1]), held_rows[None])


def solution(mesh):
    placed = (P("pipe", "dp", None), P("pipe", "dp"), P())
    return jax.shard_map(
        shards,
        mesh=mesh,
        in_specs=placed,
        out_specs=(P("pipe", "dp"), P("pipe", None, "dp", None)),
        check_vma=False,
    )
```

profile of v0, /device:TPU:0, one launch (start us, length us, event | category | flops | bytes accessed | tf_op | source)
XLA Modules:
  0.0 447.4 jit_solution(14781126711529102693)
XLA Ops:
  7.2 1.7 copy.123
  8.9 2.3 fusion.30
  11.2 3.5 copy.125
  14.8 43.2 %reduce-scatter.2.cloned.1.call-done = f32[32,3072]{1,0:T(8,128)} async-done(((f32[256,3072]{1,0:T(8,128)}), f32[32,3072]{1,0:T(8,128)}) %reduce-scatter.2.cloned.1.call-update) | async-done | bytes 393232 | tf_op jit(solution)/shard_map/reduce_scatter | solution.py:59
  58.4 31.6 %all-gather.4.cloned.1.call-done = f32[128,3072]{1,0:T(8,128)} async-done(((f32[32,3072]{1,0:T(8,128)}), f32[128,3072]{1,0:T(8,128)}) %all-gather.4.cloned.1.call-update) | async-done | bytes 1572880 | tf_op jit(solution)/shard_map/all_gather | solution.py:65
  90.0 1.7 reshape.95
  91.7 0.9 convolution_bitcast_fusion
  92.6 1.1 copy.127
  93.7 4.6 %all-to-all-start = ((f32[24,32,256]{2,1,0:T(8,128)}), f32[24,32,256]{2,1,0:T(8,128)S(1)}, u32[]{:S(2)}, u32[]{:S(2)}) async-start(f32[24,32,256]{2,1,0:T(8,128)} %copy.127), calls=%async_computation.1 | async-start | bytes 1572864 | tf_op jit(solution)/shard_map/all_to_all | solution.py:78
  98.3 0.2 all-gather.6.cloned.1.call-start
  98.6 0.7 copy.135
  99.5 0.5 iota_multiply_fusion
  100.1 0.6 iota_compare_fusion.2
  100.8 0.6 iota_compare_fusion.1
  101.4 17.8 %all-to-all-done = f32[24,32,256]{2,1,0:T(8,128)S(1)} async-done(((f32[24,32,256]{2,1,0:T(8,128)}), f32[24,32,256]{2,1,0:T(8,128)S(1)}, u32[]{:S(2)}, u32[]{:S(2)}) %all-to-all-start) | async-done | bytes 786464 | tf_op jit(solution)/shard_map/all_to_all | solution.py:78
  119.4 16.8 %copy.129 = f32[3,256,256]{0,2,1:T(8,128)} copy(f32[3,256,256]{2,1,0:T(8,128)S(1)} %bitcast.75) | data formatting | bytes 1572864 | tf_op jit(solution)/shard_map/div | solution.py:78
  136.2 0.3 copy.130
  136.5 2.3 gather_fusion
  138.9 0.6 subtract_add_fusion
  139.4 0.5 copy-done.4
  140.1 0.3 copy.131
  140.4 0.8 fusion.5
  141.3 35.2 %custom-call.16 = f32[3,128,128]{2,1,0:T(8,128)S(1)} custom-call(f32[3,128,128]{2,1,0:T(8,128)S(1)} %cholesky.122), custom_call_target="Cholesky" | custom-call | tf_op jit(solution)/shard_map/jit(cholesky)/cholesky | solution.py:17
  176.5 0.8 select_bitcast_fusion
  177.3 29.5 %custom-call.17 = f32[3,1,128,128]{2,3,1,0:T(8,128)S(1)} custom-call(f32[3,1,128,128]{3,2,1,0:T(8,128)S(1)} %select_bitcast_fusion), custom_call_target="InvertDiagBlocksLowerTriangular" | custom-call | tf_op jit(solution)/shard_map/jit(cholesky)/cholesky | solution.py:17
  206.8 0.4 constant_dynamic-update-slice_fusion.1
  207.1 0.5 convolution_subtract_fusion.1
  207.7 35.4 %custom-call.18 = f32[3,128,128]{2,1,0:T(8,128)S(1)} custom-call(f32[3,128,128]{2,1,0:T(8,128)S(1)} %convolution_subtract_fusion.1), custom_call_target="Cholesky" | custom-call | tf_op jit(solution)/shard_map/jit(cholesky)/cholesky | solution.py:17
  243.6 5.4 %while.1 = (s32[]{:T(128)}, f32[3,256,256]{2,1,0:T(8,128)S(1)}, s32[2,2]{1,0:T(2,128)S(1)}, f32[2,3,128,128]{3,2,0,1:T(8,128)}, s32[]{:T(128)}) while((s32[]{:T(128)}, f32[3,256,256]{2,1,0:T(8,128)S(1)}, s32[2,2]{1,0:T(2,128)S(1)}, f32[2,3,128,128]{3,2,0,1:T(8,128)}, s32[]{:T(128)}) %tuple.29), condition=%wide.while_cond, body=%wide.while_body.sunk | while | flops 2 | bytes 394849 | solution.py:19
  243.6 0.6 fusion.42
  244.2 2.1 bitcast_dynamic-update-slice_fusion.2
  246.2 0.6 fusion.42
  246.9 2.1 bitcast_dynamic-update-slice_fusion.2
  248.9 59.8 %custom-call.19 = f32[3,2,128,128]{2,3,1,0:T(8,128)S(1)} custom-call(f32[3,2,128,128]{3,2,1,0:T(8,128)} %bitcast.83), custom_call_target="InvertDiagBlocksLowerTriangular" | custom-call | tf_op jit(solution)/shard_map/triangular_solve | solution.py:19
  308.7 0.5 fusion.9
  309.2 0.5 convolution_subtract_fusion
  309.7 0.5 fusion.8
  310.3 1.4 convolution_multiply_fusion
  311.7 0.5 copy.140
  312.3 29.0 %all_to_all.27 = f32[3,256,256]{2,0,1:T(4,128)S(1)} all-to-all(f32[3,256,256]{2,0,1:T(4,128)S(1)} %copy.140), channel_id=1, replica_groups=mesh['pipe'=4,'dp'=8] {'dp'}, dimensions={1} | all-to-all | bytes 1572864 | tf_op jit(solution)/shard_map/all_to_all | solution.py:82
  341.4 1.0 copy.142
  342.4 0.3 all-gather.8.cloned.1.call-start
  342.7 0.7 fusion.26
  343.4 40.9 %all-gather.6.cloned.1.call-done = f32[96,32,256]{2,1,0:T(8,128)} async-done(((f32[24,32,256]{2,1,0:T(8,128)}), f32[96,32,256]{2,1,0:T(8,128)}) %all-gather.6.cloned.1.call-update) | async-done | bytes 3145744 | tf_op jit(solution)/shard_map/all_gather | solution.py:84
  384.4 4.7 %fusion = f32[12,32,256]{2,0,1:T(8,128)S(1)} fusion(f32[96,32,256]{2,1,0:T(8,128)} %all-gather.6.cloned.1.call-done, s32[12]{0:T(128)S(1)} %fusion.26), kind=kOutput, calls=%fused_computation.3 | convolution fusion | flops 113247360 | bytes 3538992 | tf_op jit(solution)/shard_map/bm,mrc->brc/dot_general | solution.py:85
  389.0 1.0 copy.144
  390.0 38.4 %all-gather.8.cloned.1.call-done = f32[12,256,256]{2,1,0:T(8,128)} async-done(((f32[12,32,256]{2,1,0:T(8,128)}), f32[12,256,256]{2,1,0:T(8,128)}) %all-gather.8.cloned.1.call-update) | async-done | bytes 3145744 | tf_op jit(solution)/shard_map/all_gather | solution.py:86
  428.4 12.5 %fusion.31 = f32[12,256,512]{2,1,0:T(8,128)} fusion(f32[12,256,256]{2,1,0:T(8,128)} %all-gather.8.cloned.1.call-done, f32[12,256,512]{2,1,0:T(8,128)} %bitcast.77), kind=kOutput, calls=%fused_computation.66 | convolution fusion | flops 4831838208 | bytes 15728640 | tf_op jit(solution)/shard_map/brk,bkc->brc/dot_general | solution.py:88
  (45 shorter events, 1.8 us)
Async XLA Ops:
  7.2 50.8 %reduce-scatter.2.cloned.1.call-start = ((), (), s32[]{:S(2)}) async-start(), calls=%async_computation.3 | async-start | bytes 3538944 | tf_op jit(solution)/shard_map/reduce_scatter | solution.py:59
  14.7 43.3 %copy-start.2 = (s32[4,12]{1,0:T(4,128)S(1)}, s32[4,12]{1,0:T(4,128)}, u32[]{:S(2)}) copy-start(s32[4,12]{1,0:T(4,128)} %param.5) | copy-start | bytes 580
  14.7 75.2 %all-gather.4.cloned.1.call-start = ((), (), s32[]{:S(2)}) async-start(), calls=%async_computation.4 | async-start | bytes 1966080 | tf_op jit(solution)/shard_map/all_gather | solution.py:65
  58.4 34.2 %copy-start.3 = (s32[4,12]{1,0:T(4,128)}, s32[4,12]{1,0:T(4,128)S(1)}, u32[]{:S(2)}) copy-start(s32[4,12]{1,0:T(4,128)S(1)} %reshape.93) | copy-start | bytes 580
  93.7 25.6 %all-to-all-start = ((f32[24,32,256]{2,1,0:T(8,128)}), f32[24,32,256]{2,1,0:T(8,128)S(1)}, u32[]{:S(2)}, u32[]{:S(2)}) async-start(f32[24,32,256]{2,1,0:T(8,128)} %copy.127), calls=%async_computation.1 | async-start | bytes 1572864 | tf_op jit(solution)/shard_map/all_to_all | solution.py:78
  98.3 286.0 %all-gather.6.cloned.1.call-start = ((), (), s32[]{:S(2)}) async-start(), calls=%async_computation.5 | async-start | bytes 3932160 | tf_op jit(solution)/shard_map/all_gather | solution.py:84
  139.4 0.5 copy-start.4
  140.4 102.9 %copy-start.1 = (pred[256,256]{1,0:T(8,128)(4,1)S(1)}, pred[256,256]{1,0:T(8,128)(4,1)}, u32[]{:S(2)}) copy-start(pred[256,256]{1,0:T(8,128)(4,1)} %iota_compare_fusion.1) | copy-start | bytes 196612
  141.2 102.3 %copy-start.6 = (s32[2]{0:T(128)S(1)}, s32[2]{0:T(128)}, u32[]{:S(2)}) copy-start(s32[2]{0:T(128)} %iota_multiply_fusion) | copy-start | bytes 28
  176.5 132.2 %copy-start = (f32[128,256]{1,0:T(8,128)S(1)}, f32[128,256]{1,0:T(8,128)}, u32[]{:S(2)}) copy-start(f32[128,256]{1,0:T(8,128)} %copy.135) | copy-start | bytes 393220
  243.3 67.0 %copy-start.5 = (f32[3]{0:T(128)S(1)}, f32[3]{0:T(128)}, u32[]{:S(2)}) copy-start(f32[3]{0:T(128)} %get-tuple-element.21) | copy-start | bytes 40
  342.4 86.0 %all-gather.8.cloned.1.call-start = ((), (), s32[]{:S(2)}) async-start(), calls=%async_computation.6 | async-start | bytes 3538944 | tf_op jit(solution)/shard_map/all_gather | solution.py:86
Sparse Core Ops, SparseCore 0:
  14.9 43.0 reduce-scatter.1
  59.8 30.0 all-gather.3
  342.5 41.7 all-gather.5
  390.1 38.1 all-gather.7
where the time goes:
time: 448 us; the launch traced here: 447 us
  waiting for transfers between devices  172 us (38%)
  other arithmetic  165 us (37%)
  local copies, waits for them, and re-layouts  37.5 us (8%)
  blocking collectives  29 us (6%)
  matrix products  24.2 us (5%)
  between operations  14.1 us (3%)
  starting transfers between devices  5.21 us (1%)
    another operation x9, other arithmetic, invert_blocks(): cholesky_lower = jnp.linalg.cholesky(shifted)  102 us
    another operation x4, other arithmetic, invert_blocks(): lax.linalg.triangular_solve(cholesky_lower, identity_stack, left_side=Tru...  61.1 us
    reduce_scatter x1, waiting for transfers between devices, shards(): lax.psum_scatter(block_terms.reshape(row_share * lax.axis_size('dp'), nbl...  43.2 us
    all_gather x1, waiting for transfers between devices, shards(): returned = lax.all_gather(held_rows, 'pipe', axis=0, tiled=True)  40.9 us
    all_gather x1, waiting for transfers between devices, shards(): inverse = lax.all_gather(own_rows, 'dp', axis=1, tiled=True)  38.4 us
    all_gather x1, waiting for transfers between devices, shards(): lax.all_gather(my_rows, 'pipe', axis=0, tiled=True)  31.6 us
    all_to_all x1, blocking collectives, shards(): lax.all_to_all(inverted, 'dp', split_axis=1, concat_axis=0, tiled=True)  29 us
    all_to_all x1, waiting for transfers between devices, shards(): lax.all_to_all(padded, 'dp', split_axis=0, concat_axis=1, tiled=True)  17.8 us
  transfers between devices with their start and end apart: 5, of which 5 were waited for; matrix products, arithmetic and copies ran while one was open for 1% of the time, Pallas kernels for 0%

commit v1 on v0

--- a/solution.py
+++ b/solution.py
@@ -6,6 +6,30 @@
 BLK = 256
 HOST = 24
 damping_ratio = 0.1
+
+
+def work_both_ways(shard, axis, dim, work, out_dim):
+    peers, index, width = (lax.axis_size(axis), lax.axis_index(axis), shard.shape[dim])
+    right = [(i, (i + 1) % peers) for i in range(peers)]
+    left = [(b, a) for a, b in right]
+    lower, upper = (lax.ppermute(shard, axis, right), lax.ppermute(shard, axis, left))
+    made = work(shard, index * width)
+    length = made.shape[out_dim]
+    out = jnp.zeros((*made.shape[:out_dim], peers * length, *made.shape[out_dim + 1 :]), made.dtype)
+
+    def put(out, made, owner):
+        return lax.dynamic_update_slice_in_dim(out, made, owner * length, axis=out_dim)
+
+    out = put(out, made, index)
+    for turn in range(1, peers // 2 + 1):
+        below, above = ((index - turn) % peers, (index + turn) % peers)
+        held = (lower, upper)
+        if turn < peers // 2:
+            lower, upper = (lax.ppermute(lower, axis, right), lax.ppermute(upper, axis, left))
+        out = put(out, work(held[0], below * width), below)
+        if 2 * turn < peers:
+            out = put(out, work(held[1], above * width), above)
+    return out
 
 
 def invert_blocks(factor, vacant):
@@ -83,9 +107,16 @@
     held_rows = spread_rows[:HOST]
     returned = lax.all_gather(held_rows, "pipe", axis=0, tiled=True)
     own_rows = jnp.einsum("bm,mrc->brc", pick_back, returned, precision=lax.Precision.HIGHEST)
-    inverse = lax.all_gather(own_rows, "dp", axis=1, tiled=True)
     grad_blocks = grad.reshape(nblocks, BLK, grad.shape[1])
-    precond = jnp.einsum("brk,bkc->brc", inverse, grad_blocks, precision=lax.Precision.HIGHEST)
+    precond = work_both_ways(
+        own_rows,
+        "dp",
+        1,
+        lambda part, start: jnp.einsum(
+            "brk,bkc->brc", part, grad_blocks, precision=lax.Precision.HIGHEST
+        ),
+        1,
+    )
     return (precond.reshape(feature_count, grad.shape[1]), held_rows[None])
 
 

time: 448 us -> 462 us (1.031)
  waiting for transfers between devices: 172 us -> 149 us
  matrix products: 24.2 us -> 42.3 us
  starting transfers between devices: 5.21 us -> 16.7 us
    all_gather x1 -> x0, waiting for transfers between devices: 38.4 us -> none  [shards(): inverse = lax.all_gather(own_rows, 'dp', axis=1, tiled=True)]
    dot_general x1 -> x8, matrix products: 12.5 us -> 32.1 us  [shards(): jnp.einsum('brk,bkc->brc', part, grad_blocks, precision=lax.Precision.HIG...]
    ppermute x0 -> x7, waiting for transfers between devices: none -> 15.3 us  [the longest x3 11.3 us: work_both_ways(): lax.ppermute(lower, axis, right)]
    ppermute x0 -> x7, starting transfers between devices: none -> 11.4 us  [the longest x2 7.47 us: work_both_ways(): lax.ppermute(upper, axis, left)]
  transfers between devices with their start and end apart: 5 -> 11, of which waited for: 5 -> 8; matrix products, arithmetic and copies ran while one was open for 1% -> 7% of each run, Pallas kernels for 0% -> 0%
where the time goes in v1:
time: 462 us; the launch traced here: 458 us
  other arithmetic  166 us (36%)
  waiting for transfers between devices  149 us (32%)
  matrix products  42.3 us (9%)
  local copies, waits for them, and re-layouts  40.8 us (9%)
  blocking collectives  29 us (6%)
  starting transfers between devices  16.7 us (4%)
  between operations  14.5 us (3%)
    another operation x9, other arithmetic, invert_blocks(): cholesky_lower = jnp.linalg.cholesky(shifted)  102 us
    another operation x4, other arithmetic, invert_blocks(): lax.linalg.triangular_solve(cholesky_lower, identity_stack, left_side=Tru...  62 us
    reduce_scatter x1, waiting for transfers between devices, shards(): lax.psum_scatter(block_terms.reshape(row_share * lax.axis_size('dp'), nbl...  43.2 us
    all_gather x1, waiting for transfers between devices, shards(): returned = lax.all_gather(held_rows, 'pipe', axis=0, tiled=True)  41.1 us
    dot_general x8, matrix products, shards(): jnp.einsum('brk,bkc->brc', part, grad_blocks, precision=lax.Precision.HIG...  32.1 us
    all_gather x1, waiting for transfers between devices, shards(): lax.all_gather(my_rows, 'pipe', axis=0, tiled=True)  31.6 us
    all_to_all x1, blocking collectives, shards(): lax.all_to_all(inverted, 'dp', split_axis=1, concat_axis=0, tiled=True)  29 us
    all_to_all x1, waiting for transfers between devices, shards(): lax.all_to_all(padded, 'dp', split_axis=0, concat_axis=1, tiled=True)  17.5 us
  transfers between devices with their start and end apart: 11, of which 8 were waited for; matrix products, arithmetic and copies ran while one was open for 7% of the time, Pallas kernels for 0%

profile of v1, /device:TPU:0, one launch (start us, length us, event | category | flops | bytes accessed | tf_op | source)
XLA Modules:
  0.0 458.4 jit_solution(13112569910328553083)
XLA Ops:
  7.2 1.7 copy.139
  8.9 2.3 fusion.37
  11.2 3.5 copy.141
  14.8 43.2 %reduce-scatter.2.cloned.1.call-done = f32[32,3072]{1,0:T(8,128)} async-done(((f32[256,3072]{1,0:T(8,128)}), f32[32,3072]{1,0:T(8,128)}) %reduce-scatter.2.cloned.1.call-update) | async-done | bytes 393232 | tf_op jit(solution)/shard_map/reduce_scatter | solution.py:83
  58.4 31.6 %all-gather.3.cloned.1.call-done = f32[128,3072]{1,0:T(8,128)} async-done(((f32[32,3072]{1,0:T(8,128)}), f32[128,3072]{1,0:T(8,128)}) %all-gather.3.cloned.1.call-update) | async-done | bytes 1572880 | tf_op jit(solution)/shard_map/all_gather | solution.py:89
  90.0 1.7 reshape.95
  91.7 0.9 convolution_bitcast_fusion
  92.6 1.1 copy.143
  93.8 4.6 %all-to-all-start = ((f32[24,32,256]{2,1,0:T(8,128)}), f32[24,32,256]{2,1,0:T(8,128)S(1)}, u32[]{:S(2)}, u32[]{:S(2)}) async-start(f32[24,32,256]{2,1,0:T(8,128)} %copy.143), calls=%async_computation.1 | async-start | bytes 1572864 | tf_op jit(solution)/shard_map/all_to_all | solution.py:102
  99.0 0.7 copy.151
  101.2 0.7 iota_compare_fusion.1
  101.8 17.5 %all-to-all-done = f32[24,32,256]{2,1,0:T(8,128)S(1)} async-done(((f32[24,32,256]{2,1,0:T(8,128)}), f32[24,32,256]{2,1,0:T(8,128)S(1)}, u32[]{:S(2)}, u32[]{:S(2)}) %all-to-all-start) | async-done | bytes 786464 | tf_op jit(solution)/shard_map/all_to_all | solution.py:102
  119.5 16.8 %copy.145 = f32[3,256,256]{0,2,1:T(8,128)} copy(f32[3,256,256]{2,1,0:T(8,128)S(1)} %bitcast.92) | data formatting | bytes 1572864 | tf_op jit(solution)/shard_map/div | solution.py:102
  136.5 2.3 gather_fusion
  140.4 0.8 fusion.3
  141.3 35.2 %custom-call.16 = f32[3,128,128]{2,1,0:T(8,128)S(1)} custom-call(f32[3,128,128]{2,1,0:T(8,128)S(1)} %cholesky.122), custom_call_target="Cholesky" | custom-call | tf_op jit(solution)/shard_map/jit(cholesky)/cholesky | solution.py:41
  176.6 0.7 select_bitcast_fusion
  177.3 29.5 %custom-call.17 = f32[3,1,128,128]{2,3,1,0:T(8,128)S(1)} custom-call(f32[3,1,128,128]{3,2,1,0:T(8,128)S(1)} %select_bitcast_fusion), custom_call_target="InvertDiagBlocksLowerTriangular" | custom-call | tf_op jit(solution)/shard_map/jit(cholesky)/cholesky | solution.py:41
  207.7 35.3 %custom-call.18 = f32[3,128,128]{2,1,0:T(8,128)S(1)} custom-call(f32[3,128,128]{2,1,0:T(8,128)S(1)} %convolution_subtract_fusion.1), custom_call_target="Cholesky" | custom-call | tf_op jit(solution)/shard_map/jit(cholesky)/cholesky | solution.py:41
  243.3 1.0 select_select_fusion
  244.3 0.7 triangular_solve.69
  245.0 5.1 %while.1 = (s32[]{:T(128)}, f32[3,256,256]{2,1,0:T(8,128)S(1)}, s32[2,2]{1,0:T(2,128)S(1)}, f32[2,3,128,128]{3,2,0,1:T(8,128)}, s32[]{:T(128)}) while((s32[]{:T(128)}, f32[3,256,256]{2,1,0:T(8,128)S(1)}, s32[2,2]{1,0:T(2,128)S(1)}, f32[2,3,128,128]{3,2,0,1:T(8,128)}, s32[]{:T(128)}) %tuple.29), condition=%wide.while_cond, body=%wide.while_body.sunk | while | flops 2 | bytes 394849 | solution.py:43
  245.6 2.0 bitcast_dynamic-update-slice_fusion.2
  248.1 2.0 bitcast_dynamic-update-slice_fusion.2
  250.1 59.8 %custom-call.19 = f32[3,2,128,128]{2,3,1,0:T(8,128)S(1)} custom-call(f32[3,2,128,128]{3,2,1,0:T(8,128)} %bitcast.99), custom_call_target="InvertDiagBlocksLowerTriangular" | custom-call | tf_op jit(solution)/shard_map/triangular_solve | solution.py:43
  311.4 1.4 convolution_multiply_fusion
  313.4 29.0 %all_to_all.27 = f32[3,256,256]{2,0,1:T(4,128)S(1)} all-to-all(f32[3,256,256]{2,0,1:T(4,128)S(1)} %copy.156), channel_id=1, replica_groups=mesh['pipe'=4,'dp'=8] {'dp'}, dimensions={1} | all-to-all | bytes 1572864 | tf_op jit(solution)/shard_map/all_to_all | solution.py:106
  342.7 1.3 copy.159
  344.2 0.7 fusion.33
  344.9 41.1 %all-gather.5.cloned.1.call-done = f32[96,32,256]{2,0,1:T(8,128)} async-done(((f32[24,32,256]{2,0,1:T(8,128)}), f32[96,32,256]{2,0,1:T(8,128)}) %all-gather.5.cloned.1.call-update) | async-done | bytes 3145744 | tf_op jit(solution)/shard_map/all_gather | solution.py:108
  386.0 3.2 fusion.28
  389.4 3.5 collective-permute-start.1
  393.0 0.8 broadcast_in_dim.14
  393.7 5.8 %convolution_dynamic-update-slice_fusion.7 = f32[12,256,512]{2,1,0:T(8,128)S(1)} fusion(f32[12,256,512]{2,1,0:T(8,128)S(1)} %broadcast_in_dim.14, s32[]{:T(128)S(6)} %select_n.74, f32[12,256,512]{2,1,0:T(8,128)} %bitcast.79, f32[12,32,256]{2,0,1:T(8,128)S(1)} %fusion.28), kind=kOutput, calls=%fused_computation.10 | convolution fusion | flops 603979776 | bytes 7602180 | tf_op jit(solution)/shard_map/brk,bkc->brc/dot_general | solution.py:115
  399.6 4.0 collective-permute-done
  403.6 3.5 collective-permute-start.3
  407.2 3.8 convolution_dynamic-update-slice_fusion.6
  410.9 3.8 convolution_dynamic-update-slice_fusion.5
  414.7 4.9 %collective-permute-done.2 = f32[12,32,256]{2,0,1:T(8,128)S(1)} collective-permute-done((f32[12,32,256]{2,0,1:T(8,128)S(1)}, f32[12,32,256]{2,0,1:T(8,128)S(1)}, u32[]{:S(2)}, u32[]{:S(2)}) %collective-permute-start.2) | collective-permute-done | bytes 393248 | tf_op jit(solution)/shard_map/ppermute | solution.py:28
  419.6 3.9 collective-permute-start.5
  423.5 3.8 convolution_dynamic-update-slice_fusion.4
  427.3 3.8 convolution_dynamic-update-slice_fusion.3
  431.1 3.6 collective-permute-done.4
  434.8 3.8 convolution_dynamic-update-slice_fusion.2
  438.6 3.8 convolution_dynamic-update-slice_fusion.1
  442.3 2.8 collective-permute-done.6
  445.2 3.8 convolution_dynamic-update-slice_fusion
  449.0 2.7 copy-done
  (69 shorter events, 9.6 us)
Async XLA Ops:
  7.2 50.8 %reduce-scatter.2.cloned.1.call-start = ((), (), s32[]{:S(2)}) async-start(), calls=%async_computation.3 | async-start | bytes 3538944 | tf_op jit(solution)/shard_map/reduce_scatter | solution.py:83
  11.2 46.8 %copy-start.3 = (s32[4,12]{1,0:T(4,128)S(1)}, s32[4,12]{1,0:T(4,128)}, u32[]{:S(2)}) copy-start(s32[4,12]{1,0:T(4,128)} %param.5) | copy-start | bytes 580
  14.8 75.3 %all-gather.3.cloned.1.call-start = ((), (), s32[]{:S(2)}) async-start(), calls=%async_computation.4 | async-start | bytes 1966080 | tf_op jit(solution)/shard_map/all_gather | solution.py:89
  58.4 61.0 %copy-start.4 = (s32[4,12]{1,0:T(4,128)}, s32[4,12]{1,0:T(4,128)S(1)}, u32[]{:S(2)}) copy-start(s32[4,12]{1,0:T(4,128)S(1)} %reshape.93) | copy-start | bytes 580
  93.8 25.6 %all-to-all-start = ((f32[24,32,256]{2,1,0:T(8,128)}), f32[24,32,256]{2,1,0:T(8,128)S(1)}, u32[]{:S(2)}, u32[]{:S(2)}) async-start(f32[24,32,256]{2,1,0:T(8,128)} %copy.143), calls=%async_computation.1 | async-start | bytes 1572864 | tf_op jit(solution)/shard_map/all_to_all | solution.py:102
  98.4 287.6 %all-gather.5.cloned.1.call-start = ((), (), s32[]{:S(2)}) async-start(), calls=%async_computation.5 | async-start | bytes 3932160 | tf_op jit(solution)/shard_map/all_gather | solution.py:108
  139.5 0.5 copy-start.5
  140.4 169.4 %copy-start.2 = (f32[128,256]{1,0:T(8,128)S(1)}, f32[128,256]{1,0:T(8,128)}, u32[]{:S(2)}) copy-start(f32[128,256]{1,0:T(8,128)} %copy.151) | copy-start | bytes 393220
  141.3 170.2 %copy-start.6 = (f32[3]{0:T(128)S(1)}, f32[3]{0:T(128)}, u32[]{:S(2)}) copy-start(f32[3]{0:T(128)} %get-tuple-element.21) | copy-start | bytes 40
  342.6 56.9 %copy-start.1 = (f32[8,3,32,256]{3,2,1,0:T(8,128)}, f32[8,3,32,256]{3,2,1,0:T(8,128)S(1)}, u32[]{:S(2)}) copy-start(f32[8,3,32,256]{3,2,1,0:T(8,128)S(1)} %copy.158) | copy-start | bytes 2359300
  386.0 21.2 %slice-start = ((s8[6291456]{0:T(1024)(128)(4,1)}), s8[4194304]{0:T(1024)(128)(4,1)S(1)}, s32[]{:S(2)}) async-start(s8[6291456]{0:T(1024)(128)(4,1)} %bitcast.80), calls=%async_computation.6 | async-start | bytes 8388608
  389.1 14.5 %collective-permute-start = (f32[12,32,256]{2,0,1:T(8,128)S(1)}, f32[12,32,256]{2,0,1:T(8,128)S(1)}, u32[]{:S(2)}, u32[]{:S(2)}) collective-permute-start(f32[12,32,256]{2,0,1:T(8,128)S(1)} %fusion.28), channel_id=1, source_target_pairs={{0,1},{1,2},{2,3},{3,4},{4,5},{5,6},{6,7},{7,0},{8,9},{9,10},{10,1... | collective-permute-start | bytes 1179656 | tf_op jit(solution)/shard_map/ppermute | solution.py:15
  389.4 14.2 %collective-permute-start.1 = (f32[12,32,256]{2,0,1:T(8,128)S(1)}, f32[12,32,256]{2,0,1:T(8,128)S(1)}, u32[]{:S(2)}, u32[]{:S(2)}) collective-permute-start(f32[12,32,256]{2,0,1:T(8,128)S(1)} %fusion.28), channel_id=1, source_target_pairs={{1,0},{2,1},{3,2},{4,3},{5,4},{6,5},{7,6},{0,7},{9,8},{10,9},{11,1... | collective-permute-start | bytes 1179656 | tf_op jit(solution)/shard_map/ppermute | solution.py:15
  392.9 14.2 %slice-start.1 = ((s8[6291456]{0:T(1024)(128)(4,1)}), s8[2097152]{0:T(1024)(128)(4,1)S(1)}, s32[]{:S(2)}) async-start(s8[6291456]{0:T(1024)(128)(4,1)} %bitcast.80), calls=%async_computation.7 | async-start | bytes 4194304
  403.6 16.0 %collective-permute-start.2 = (f32[12,32,256]{2,0,1:T(8,128)S(1)}, f32[12,32,256]{2,0,1:T(8,128)S(1)}, u32[]{:S(2)}, u32[]{:S(2)}) collective-permute-start(f32[12,32,256]{2,0,1:T(8,128)S(1)} %collective-permute-done), channel_id=1, source_target_pairs={{0,1},{1,2},{2,3},{3,4},{4,5},{5,6},{6,7},{7,0},{8,9},{9,10},{10,1... | collective-permute-start | bytes 1179656 | tf_op jit(solution)/shard_map/ppermute | solution.py:28
  403.6 16.0 %collective-permute-start.3 = (f32[12,32,256]{2,0,1:T(8,128)S(1)}, f32[12,32,256]{2,0,1:T(8,128)S(1)}, u32[]{:S(2)}, u32[]{:S(2)}) collective-permute-start(f32[12,32,256]{2,0,1:T(8,128)S(1)} %collective-permute-done.1), channel_id=1, source_target_pairs={{1,0},{2,1},{3,2},{4,3},{5,4},{6,5},{7,6},{0,7},{9,8},{10,9},{11,1... | collective-permute-start | bytes 1179656 | tf_op jit(solution)/shard_map/ppermute | solution.py:28
  419.6 15.0 %collective-permute-start.4 = (f32[12,32,256]{2,0,1:T(8,128)S(1)}, f32[12,32,256]{2,0,1:T(8,128)S(1)}, u32[]{:S(2)}, u32[]{:S(2)}) collective-permute-start(f32[12,32,256]{2,0,1:T(8,128)S(1)} %collective-permute-done.2), channel_id=1, source_target_pairs={{0,1},{1,2},{2,3},{3,4},{4,5},{5,6},{6,7},{7,0},{8,9},{9,10},{10,1... | collective-permute-start | bytes 1179656 | tf_op jit(solution)/shard_map/ppermute | solution.py:28
  419.6 19.0 %collective-permute-start.5 = (f32[12,32,256]{2,0,1:T(8,128)S(1)}, f32[12,32,256]{2,0,1:T(8,128)S(1)}, u32[]{:S(2)}, u32[]{:S(2)}) collective-permute-start(f32[12,32,256]{2,0,1:T(8,128)S(1)} %collective-permute-done.3), channel_id=1, source_target_pairs={{1,0},{2,1},{3,2},{4,3},{5,4},{6,5},{7,6},{0,7},{9,8},{10,9},{11,1... | collective-permute-start | bytes 1179656 | tf_op jit(solution)/shard_map/ppermute | solution.py:28
  434.6 10.6 %collective-permute-start.6 = (f32[12,32,256]{2,0,1:T(8,128)S(1)}, f32[12,32,256]{2,0,1:T(8,128)S(1)}, u32[]{:S(2)}, u32[]{:S(2)}) collective-permute-start(f32[12,32,256]{2,0,1:T(8,128)S(1)} %collective-permute-done.4), channel_id=1, source_target_pairs={{0,1},{1,2},{2,3},{3,4},{4,5},{5,6},{6,7},{7,0},{8,9},{9,10},{10,1... | collective-permute-start | bytes 1179656 | tf_op jit(solution)/shard_map/ppermute | solution.py:28
  449.0 2.7 copy-start
Sparse Core Ops, SparseCore 0:
  14.9 43.0 reduce-scatter.1
  59.8 30.1 all-gather.2
  344.1 41.7 all-gather.4
